TPU v7x, 32 devices: a whole 2x2x4 slice. The times are simulated.
32 devices in a mesh: members: 2 (over x), zonal: 8 (over z, y), merid: 2 (over core).
Axes of the slice: x: 2, y: 2, z: 4, core: 2. Of those that a mesh axis runs over, the one named last changes fastest.
Arguments:
- height: float32 [256, 1024], P(('members', 'zonal'), 'merid'), parts along dimension 0, may hold values from -6 to 6
- transport_u: float32 [256, 1024], P(('members', 'zonal'), 'merid'), parts along dimension 0, may hold values from -4 to 4
- transport_v: float32 [256, 1024], P(('members', 'zonal'), 'merid'), parts along dimension 0, may hold values from -4 to 4
- thickness: float32 [14, 256, 1024], P(None, ('members', 'zonal'), 'merid'), parts along dimension 1, may hold values from 0.5 to 2
- velocity_u: float32 [14, 256, 1024], P(None, ('members', 'zonal'), 'merid'), parts along dimension 1, may hold values from -3 to 3
- velocity_v: float32 [14, 256, 1024], P(None, ('members', 'zonal'), 'merid'), parts along dimension 1, may hold values from -3 to 3
- sea_faces: int32 [2, 128, 1024], P(None, 'zonal', 'merid'), may hold values 0 or 1
- wind_seeds: int32 [8, 2], P('members'), parts along dimension 0, may hold values from 1 to 96
- wind_scale: float32 [8], P('members'), parts along dimension 0, may hold values from 0.5 to 2
- wind_base: float32 [2, 128, 1024], P(None, 'zonal', 'merid'), may hold values from -6 to 6
Outputs:
- final_height: float32 [256, 1024], P(('members', 'zonal'), 'merid'), parts along dimension 0
- final_transport_u: float32 [256, 1024], P(('members', 'zonal'), 'merid'), parts along dimension 0
- final_transport_v: float32 [256, 1024], P(('members', 'zonal'), 'merid'), parts along dimension 0
- final_thickness: float32 [14, 256, 1024], P(None, ('members', 'zonal'), 'merid'), parts along dimension 1
- final_velocity_u: float32 [14, 256, 1024], P(None, ('members', 'zonal'), 'merid'), parts along dimension 1
- final_velocity_v: float32 [14, 256, 1024], P(None, ('members', 'zonal'), 'merid'), parts along dimension 1
There are 2 independent parts, one for each index of `members`. A program takes and returns all parts, laid end to end along the dimension named above; an argument that names none is the same for every part. Nothing has to cross between parts.
All inputs are finite; a program needn't handle non-finite values. No bound on the sum of `sea_faces` on one device may be relied on, other than what follows from the above.
Results may differ from a plain program's by a relative error of at most 0.0001.
Values sent between devices are 32-bit elements; how exact they have to be, the bound alone decides.
A program may use at most 64 MiB of HBM per device.

v0:
```python
import functools
import math

import jax
import jax.numpy as jnp
from jax import lax
from jax.experimental import pallas as pl
from jax.experimental.pallas import tpu as pltpu
from jax.sharding import PartitionSpec as P

NSUB = 6
STEPS = 2
MARGIN = NSUB
PAD = 8

WAVE_LIMIT = 0.225
STRESS_SCALE = 0.1
FLUX_STEP = 0.05
PRESS_COEF = 0.05
LANES = 128
VMEM_BYTES = 67043328
SPARE = 1 << 15
FIELDS = 8
SLOT = LANES // FIELDS
WEST = (NSUB - 1, NSUB, NSUB - 1, NSUB - 1, NSUB - 2, NSUB - 1, NSUB - 1, NSUB - 2)
EAST = (NSUB, NSUB, NSUB) + (NSUB - 1,) * 5
ORDER = (0, 1, 2, 3, 4, 6, 7, 5)
CUT = 32
PIECES = 2
MESH = pl.DeviceIdType.MESH


def roll(value, shift, axis):
    return pltpu.roll(value, shift % value.shape[axis], axis)


def iota(shape, axis):
    return lax.broadcasted_iota(jnp.int32, shape, axis)


def turns(seed, index, total):
    part = seed * index * (1.0 / total)
    angle = (2.0 * math.pi) * (part - jnp.floor(part))
    return jnp.cos(angle), jnp.sin(angle)


def tile_up(count):
    return -(-count // 8) * 8


def layer_trial(h_ref, u_ref, v_ref, o_h, o_u, o_v, sums, deep):
    layers, nx, ny = h_ref.shape
    at_east = iota((nx, ny), 0) == nx - 1
    at_north = iota((nx, ny), 1) == ny - 1
    zero = jnp.zeros((nx, ny), jnp.float32)
    press_u, press_v, sum_u, sum_v = zero, zero, zero, zero
    deep_u, deep_v = zero, zero
    for l in range(layers):
        h, u, v = h_ref[l], u_ref[l], v_ref[l]
        h_east, h_north = roll(h, -1, 0), roll(h, -1, 1)
        hu = (h + h_east) * 0.5
        hv = (h + h_north) * 0.5
        if deep:
            deep_u = deep_u + hu
            deep_v = deep_v + hv
        flux_u = jnp.where(at_east, 0.0, u * hu)
        flux_v = jnp.where(at_north, 0.0, v * hv)
        press_u = press_u + (h_east - h)
        press_v = press_v + (h_north - h)
        trial_u = u - PRESS_COEF * press_u
        trial_v = v - PRESS_COEF * press_v
        sum_u = sum_u + hu * trial_u
        sum_v = sum_v + hv * trial_v
        o_u[l] = trial_u
        o_v[l] = trial_v
        o_h[l] = h - FLUX_STEP * (flux_u - roll(flux_u, 1, 0) + flux_v - roll(flux_v, 1, 1))
    sums[0] = sum_u
    sums[1] = sum_v
    if deep:
        sums[2] = deep_u
        sums[3] = deep_v


def layer_edges(h_ref, v_ref, own_r, own_l, recv_w, recv_e, packs, o_h, o_u, o_v, sums, top, deep):
    layers, nx, ny = h_ref.shape
    up = own_l.shape[0]
    layer = iota((up, ny), 0)
    h_last, u_last, h_first = own_r[0:up], own_r[up:], own_l[...]
    h_e, h_w, u_w = recv_e[...], recv_w[0:up], recv_w[up:]
    hu = (h_last + h_e) * 0.5
    press = h_e - h_last
    step = 1
    while step < layers:
        press = press + jnp.where(layer >= step, roll(press, step, 0), 0.0)
        step *= 2
    trial = u_last - PRESS_COEF * press
    outflow = FLUX_STEP * (u_last * hu)
    inflow = FLUX_STEP * (u_w * ((h_w + h_first) * 0.5))
    whole = lambda a: jnp.sum(jnp.where(layer < layers, a, 0.0), axis=0, keepdims=True)
    sums[0, nx - 1 : nx, :] = whole(hu * trial)
    if deep:
        sums[2, nx - 1 : nx, :] = whole(hu)
    for l in range(layers):
        o_u[l, nx - 1 : nx, :] = trial[l : l + 1]
        o_h[l, nx - 1 : nx, :] = o_h[l, nx - 1 : nx, :] - outflow[l : l + 1]
        o_h[l, 0:1, :] = o_h[l, 0:1, :] + inflow[l : l + 1]

    lane = iota((nx, LANES), 1)
    last = ny - LANES
    at_end = lane == LANES - 1
    at_start = jnp.logical_and(top, lane == 0)
    side = packs[0]
    cap = jnp.where(top, packs[1], side)
    press, total, deep_v = 0.0, 0.0, 0.0
    for l in range(layers):
        h, v = h_ref[l, :, last:ny], v_ref[l, :, last:ny]
        h_north = roll(cap, LANES - 1 - l, 1)
        hv = (h + h_north) * 0.5
        press = press + (h_north - h)
        trial = v - PRESS_COEF * press
        total = total + hv * trial
        deep_v = deep_v + hv
        o_v[l, :, last:ny] = jnp.where(at_end, trial, o_v[l, :, last:ny])
        o_h[l, :, last:ny] = o_h[l, :, last:ny] - jnp.where(at_end, FLUX_STEP * (v * hv), 0.0)
        h_south, v_south = roll(side, -l, 1), roll(side, -(layers + l), 1)
        inflow = FLUX_STEP * (v_south * ((h_south + h_ref[l, :, 0:LANES]) * 0.5))
        o_h[l, :, 0:LANES] = o_h[l, :, 0:LANES] + jnp.where(at_start, inflow, 0.0)
    sums[1, :, last:ny] = jnp.where(at_end, total, sums[1, :, last:ny])
    if deep:
        sums[3, :, last:ny] = jnp.where(at_end, deep_v, sums[3, :, last:ny])


def layer_close(o_u, o_v, sums, mean, masks, depth, deep):
    if deep:
        depth[0] = 1.0 / sums[2]
        depth[1] = 1.0 / sums[3]
    for k, out in enumerate((o_u, o_v)):
        fix = (mean[k] * (1.0 / NSUB) - sums[k]) * depth[k]
        mask = masks[k]
        for l in range(out.shape[0]):
            out[l] = mask * (out[l] + fix)


def last_kernel(flat, n_h, n_u, n_v, o_eta, o_bu, o_bv, o_h, o_u, o_v, sems):
    layers = n_h.shape[0]
    moves = [(flat.at[k], o) for k, o in enumerate((o_eta, o_bu, o_bv))]
    cut = layers // PIECES
    for n, o in ((n_h, o_h), (n_u, o_u), (n_v, o_v)):
        for p in range(PIECES):
            part = slice(p * cut, layers if p == PIECES - 1 else (p + 1) * cut)
            moves.append((n.at[part], o.at[part]))
    copies = [pltpu.make_async_copy(src, dst, sems.at[k]) for k, (src, dst) in enumerate(moves)]
    for copy in copies:
        copy.start()
    for copy in copies:
        copy.wait()


def kernel(
    zonal_devices,
    merid_devices,
    height_any,
    trans_u_any,
    trans_v_any,
    thick_any,
    vel_u_any,
    vel_v_any,
    faces_any,
    seeds_any,
    scale_any,
    base_any,
    flat,
    o_h,
    o_u,
    o_v,
    thick,
    vel_u,
    vel_v,
    faces,
    seeds,
    scale,
    mid_h,
    mid_u,
    mid_v,
    mean,
    sums,
    depth,
    X,
    G,
    D,
    F,
    wind_own,
    wind_far,
    west_send,
    west_recv,
    east_send,
    east_recv,
    pack_send,
    inner_recv,
    fold_recv,
    lay_send_r,
    lay_send_l,
    lay_recv_w,
    lay_recv_e,
    lay_pack_send,
    lay_pack_recv,
    load_sem,
    send_sem,
    recv_sem,
    lay_send_sem,
    lay_recv_sem,
    late_sem,
):
    layers, nx, ny = thick.shape
    Z = zonal_devices
    total_x, total_y = nx * Z, ny * merid_devices
    z = lax.axis_index("zonal")
    m = lax.axis_index("merid")
    other = 1 - m
    bottom = m == 0
    top = m == merid_devices - 1
    right, left = lax.rem(z + 1, Z), lax.rem(z + Z - 1, Z)
    mirror = Z - 1 - z
    mirror_e, mirror_w = lax.rem(mirror + 1, Z), lax.rem(mirror + Z - 1, Z)
    rows = nx + 2 * PAD
    width = ny + LANES
    last = ny - LANES
    own = slice(PAD, PAD + nx)
    lane = iota((nx, LANES), 1)

    barrier = pltpu.get_barrier_semaphore()
    first_z, last_z = z == 0, z == Z - 1
    mirrors = (mirror_w, mirror, mirror_e)

    def greet(sem, zz, mm):
        pl.semaphore_signal(sem, inc=1, device_id={"zonal": zz, "merid": mm}, device_id_type=MESH)

    greet(barrier, z, other)
    for mm in (m, other):
        greet(barrier, left, mm)

        @pl.when(jnp.logical_not(last_z))
        def _():
            greet(barrier, right, mm)

    for zz in mirrors:

        @pl.when(jnp.logical_and(top, zz > z))
        def _():
            greet(barrier, zz, m)

    moves = (
        (faces_any, faces),
        (height_any, X.at[0, own, 0:ny]),
        (trans_u_any, X.at[1, own, 0:ny]),
        (trans_v_any, X.at[2, own, 0:ny]),
        (base_any, X.at[6:8, own, 0:ny]),
        (thick_any, thick),
        (vel_u_any, vel_u),
        (vel_v_any, vel_v),
        (seeds_any, seeds),
        (scale_any, scale),
    )
    loads = [pltpu.make_async_copy(src, dst, load_sem.at[k]) for k, (src, dst) in enumerate(moves)]
    for load in loads:
        load.start()

    near = 3 + jnp.where(first_z, 0, 2)
    lower = sum((zz < z).astype(jnp.int32) for zz in mirrors)
    upper = sum((zz > z).astype(jnp.int32) for zz in mirrors)
    pl.semaphore_wait(barrier, near + jnp.where(top, lower, 0))

    @pl.when(last_z)
    def _():
        for mm in (m, other):
            greet(late_sem.at[0], right, mm)

    for zz in mirrors:

        @pl.when(jnp.logical_and(top, zz < z))
        def _():
            greet(late_sem.at[1], zz, m)

    loads[0].wait()
    X[3, own, 0:ny] = faces[0].astype(jnp.float32)
    X[4, own, 0:ny] = faces[1].astype(jnp.float32)
    for load in loads[1:5]:
        load.wait()

    def pack_rows(step, start, stop):
        west = sum(WEST[f] for f in ORDER[:start])
        east = sum(EAST[f] for f in ORDER[:start])
        for f in ORDER[start:stop]:
            west_send[step, west : west + WEST[f], :] = X[f, PAD + nx - WEST[f] : PAD + nx, 0:ny]
            east_send[step, east : east + EAST[f], :] = X[f, PAD : PAD + EAST[f], 0:ny]
            west += WEST[f]
            east += EAST[f]

    def pack_edges(step, fields):
        inner = jnp.zeros((nx, LANES), jnp.float32)
        crest = jnp.zeros((nx, LANES), jnp.float32)
        for f in range(fields):
            here = jnp.logical_and(lane >= f * SLOT, lane < (f + 1) * SLOT)
            high = roll(X[f, own, last:ny], SLOT * (f + 1), 1)
            low = roll(X[f, own, 0:LANES], SLOT * f, 1)
            crest = jnp.where(here, high, crest)
            inner = jnp.where(here, jnp.where(bottom, high, low), inner)
        pack_send[step, 0] = inner
        pack_send[step, 2] = crest
        for r in range(nx):
            pack_send[step, 1, r : r + 1, :] = pack_send[step, 2, nx - 1 - r : nx - r, :]

    def send_tile(step, fields):
        def send(src, dst, k, zz, mm):
            return pltpu.make_async_remote_copy(
                src_ref=src,
                dst_ref=dst,
                send_sem=send_sem.at[step, k],
                recv_sem=recv_sem.at[step, k],
                device_id={"zonal": zz, "merid": mm},
                device_id_type=MESH,
            )

        def rows_of(src, dst, k, zz, count):
            cuts = [0, CUT, count] if count > CUT else [0, count]
            parts = [slice(low, high) for low, high in zip(cuts[:-1], cuts[1:])]
            return [send(src.at[step, p], dst.at[step, p], k + 2 * n, zz, m) for n, p in enumerate(parts)]

        tail, whole, start = slice(nx - PAD, nx), slice(0, nx), slice(0, PAD)
        places = (slice(0, PAD), own, slice(PAD + nx, rows))
        inner = lambda s, part: (pack_send.at[step, 0, part], inner_recv.at[step, places[s]])
        west = rows_of(west_send, west_recv, 0, right, tile_up(sum(WEST[:fields])))
        east = rows_of(east_send, east_recv, 1, left, tile_up(sum(EAST[:fields])))
        west.append(send(*inner(0, tail), 6, right, other))
        east.append(send(*inner(2, start), 4, left, other))
        across = send(*inner(1, whole), 5, z, other)
        folds = []
        for s, part, zz in ((2, start, mirror_w), (1, whole, mirror), (0, tail, mirror_e)):
            src, dst = pack_send.at[step, 1, part], fold_recv.at[step, places[s]]
            near = pltpu.make_async_copy(src, dst, recv_sem.at[step, 7 + s])
            folds.append((send(src, dst, 7 + s, zz, m), near, zz))
        return west, east, across, folds

    even = lax.rem(z, 2) == 0

    def start_all(copies):
        for copy in copies:
            copy.start()

    far_west, far_east = jnp.logical_not(even), jnp.logical_and(even, jnp.logical_not(first_z))

    def each(west_when, east_when, act, tile):
        pl.when(west_when)(lambda: act(tile[0]))
        pl.when(east_when)(lambda: act(tile[1]))

    def start_folds(folds, chosen):
        for far_copy, _, zz in folds:
            pl.when(jnp.logical_and(top, chosen(zz)))(far_copy.start)

    def take_tile(step, fields, west_copies, east_copies, across, folds):
        for copy in west_copies + east_copies + [across]:
            copy.wait()
        for far_copy, near_copy, zz in folds:

            @pl.when(jnp.logical_and(top, zz != z))
            def _():
                far_copy.wait()

            @pl.when(jnp.logical_and(top, zz == z))
            def _():
                near_copy.wait()

        west = east = 0
        for f in ORDER[:fields]:
            X[f, PAD - WEST[f] : PAD, 0:ny] = west_recv[step, west : west + WEST[f], :]
            X[f, PAD + nx : PAD + nx + EAST[f], 0:ny] = east_recv[step, east : east + EAST[f], :]
            west += WEST[f]
            east += EAST[f]
        for f in range(fields):
            got = inner_recv[step]
            X[f, :, ny:width] = jnp.where(
                top, roll(got, LANES - SLOT * (f + 1), 1), roll(got, LANES - SLOT * f, 1)
            )
            G[f] = roll(fold_recv[step], LANES - SLOT * (f + 1), 1)

    pack_rows(0, 0, FIELDS - 1)
    tile = send_tile(0, FIELDS)
    lead = (jnp.logical_or(far_west, first_z), far_east)
    each(*lead, lambda c: c[0].start(), tile)
    loads[5].wait()
    total = thick[0]
    for l in range(1, layers):
        total = total + thick[l]
    X[5, own, 0:ny] = (WAVE_LIMIT / layers) * total
    pack_rows(0, FIELDS - 1, FIELDS)
    pack_edges(0, FIELDS)
    each(*lead, lambda c: start_all(c[1:]), tile)
    each(far_east, far_west, start_all, tile)
    tile[2].start()
    start_folds(tile[3], lambda zz: zz < z)
    for _, near_copy, zz in tile[3]:
        pl.when(jnp.logical_and(top, zz == z))(near_copy.start)

    def lay_copies(step):
        def one(src, dst, k, zz, mm):
            return pltpu.make_async_remote_copy(
                src_ref=src,
                dst_ref=dst,
                send_sem=lay_send_sem.at[step, k],
                recv_sem=lay_recv_sem.at[step, k],
                device_id={"zonal": zz, "merid": mm},
                device_id_type=MESH,
            )

        return [
            one(lay_send_r.at[step], lay_recv_w.at[step], 0, right, m),
            one(lay_send_l.at[step], lay_recv_e.at[step], 1, left, m),
            one(lay_pack_send.at[step, 0], lay_pack_recv.at[step, 0], 2, z, other),
            one(lay_pack_send.at[step, 1], lay_pack_recv.at[step, 1], 3, mirror, m),
        ]

    above = lay_send_r.shape[1] // 2

    def send_layers(step, h_ref, u_ref, v_ref):
        edge = jnp.zeros((nx, LANES), jnp.float32)
        brim = jnp.zeros((nx, LANES), jnp.float32)
        for l in range(layers):
            lay_send_r[step, l : l + 1, :] = h_ref[l, nx - 1 : nx, :]
            lay_send_r[step, above + l : above + l + 1, :] = u_ref[l, nx - 1 : nx, :]
            lay_send_l[step, l : l + 1, :] = h_ref[l, 0:1, :]
            high = roll(h_ref[l, :, last:ny], l + 1, 1)
            low = roll(h_ref[l, :, 0:LANES], l, 1)
            high_v = roll(v_ref[l, :, last:ny], layers + l + 1, 1)
            edge = jnp.where(lane == l, jnp.where(bottom, high, low), edge)
            edge = jnp.where(lane == layers + l, high_v, edge)
            brim = jnp.where(lane == l, high, brim)
        lay_pack_send[step, 0] = edge
        lay_pack_send[step, 2] = brim
        for r in range(nx):
            lay_pack_send[step, 1, r : r + 1, :] = lay_pack_send[step, 2, nx - 1 - r : nx - r, :]
        return lay_copies(step)

    def start_layers(out, first):
        out[2].start()
        late_left, late_fold = (first_z, mirror > z) if first else (False, False)
        pl.when(jnp.logical_and(top, jnp.logical_not(late_fold)))(out[3].start)
        pl.when(far_west)(lambda: start_all(out[:2]))
        pl.when(jnp.logical_and(even, jnp.logical_not(late_left)))(lambda: start_all(out[1::-1]))
        if first:
            pl.when(first_z)(out[0].start)

    def wait_layers(out):
        for copy in out[:3]:
            copy.wait()

        @pl.when(top)
        def _():
            out[3].wait()

    for load in loads[6:]:
        load.wait()
    out = send_layers(0, thick, vel_u, vel_v)

    start_layers(out, True)
    first = (z * nx - PAD).astype(jnp.float32)
    col = first + iota((rows, 1), 0).astype(jnp.float32) + float(total_x)
    far_col = float(2 * total_x - 1) - (first + iota((rows, 1), 0).astype(jnp.float32))
    spot = iota((1, width), 1)
    row = spot + m * ny
    row = jnp.where(jnp.logical_and(top, spot >= ny), row - width, row).astype(jnp.float32)
    far_row = (iota((1, LANES), 1) + (total_y - LANES)).astype(jnp.float32)
    px = jnp.zeros((rows, width), jnp.float32)
    py = jnp.zeros((rows, width), jnp.float32)
    fx = jnp.zeros((rows, LANES), jnp.float32)
    fy = jnp.zeros((rows, LANES), jnp.float32)
    for k in range(seeds.shape[1]):
        seed_x = seeds[0, k].astype(jnp.float32)
        seed_y = seeds[1, k].astype(jnp.float32)
        ca, sa = turns(seed_x, col, total_x)
        cf, sf = turns(seed_x, far_col, total_x)
        cb, sb = turns(seed_y, row, total_y)
        cg, sg = turns(seed_y, far_row, total_y)
        amp = scale[k]
        ca, sa, cf, sf = amp * ca, amp * sa, amp * cf, amp * sf
        px = px + (ca * cb - sa * sb)
        py = py + (sa * cb + ca * sb)
        fx = fx + (cf * cg - sf * sg)
        fy = fy + (sf * cg + cf * sg)
    wind_own[0] = px
    wind_own[1] = py
    wind_far[0] = fx
    wind_far[1] = fy

    layer_trial(thick, vel_u, vel_v, mid_h, mid_u, mid_v, sums, True)

    @pl.when(first_z)
    def _():
        pl.semaphore_wait(late_sem.at[0], 2)
        start_all(tile[1])


    @pl.when(jnp.logical_and(top, upper > 0))
    def _():
        pl.semaphore_wait(late_sem.at[1], upper)

    start_folds(tile[3], lambda zz: zz > z)
    pl.when(first_z)(out[1].start)
    pl.when(jnp.logical_and(top, mirror > z))(out[3].start)

    take_tile(0, FIELDS, *tile)
    for k in range(2):
        X[6 + k] = STRESS_SCALE * (X[6 + k] + wind_own[k])
        G[6 + k] = STRESS_SCALE * (G[6 + k] + wind_far[k])

    lanes = iota((rows, width), 1)
    wall = jnp.logical_and(bottom, lanes == 0)
    crown = jnp.logical_and(top, lanes == ny - 1)
    far_top = iota((rows, LANES), 1) == LANES - 1

    def close_step(step, h_ref, v_ref, n_h, n_u, n_v):
        layer_edges(
            h_ref, v_ref, lay_send_r.at[step], lay_send_l.at[step], lay_recv_w.at[step], lay_recv_e.at[step],
            lay_pack_recv.at[step], n_h, n_u, n_v, sums, top, step == 0,
        )
        layer_close(n_u, n_v, sums, mean, masks, depth, step == 0)

    def substep(carry):
        eta, bu, bv, south_v, g_eta, g_bu, g_bv, g_south_v = carry
        eta = eta - (bu - roll(bu, 1, 0) + bv - south_v)
        g_eta = g_eta - (g_bu - roll(g_bu, -1, 0) + g_bv - g_south_v)
        north, south = roll(eta, -1, 1), roll(eta, 1, 1)
        north = jnp.where(crown, g_eta[:, LANES - 1 :], north)
        g_north = jnp.where(far_top, eta[:, ny - 1 : ny], roll(g_eta, -1, 1))
        g_south = roll(g_eta, 1, 1)
        bu = X[3] * (bu - X[5] * (roll(eta, -1, 0) - eta) + X[6])
        bv = X[4] * (bv - X[5] * (north - eta) + X[7])
        south_v = jnp.where(wall, 0.0, D[0] * (south_v - D[1] * (eta - south) + D[2]))
        g_bu = G[3] * (g_bu - G[5] * (roll(g_eta, 1, 0) - g_eta) + G[6])
        g_bv = G[4] * (g_bv - G[5] * (g_north - g_eta) + G[7])
        g_south_v = F[0] * (g_south_v - F[1] * (g_eta - g_south) + F[2])
        mean[0] = mean[0] + bu[own, 0:ny]
        mean[1] = mean[1] + bv[own, 0:ny]
        return eta, bu, bv, south_v, g_eta, g_bu, g_bv, g_south_v

    def substeps():
        mean[...] = jnp.zeros((2, nx, ny), jnp.float32)
        bv, g_bv = X[2], G[2]
        carry = X[0], X[1], bv, jnp.where(wall, 0.0, roll(bv, 1, 1)), G[0], G[1], g_bv, roll(g_bv, 1, 1)
        for _ in range(NSUB):
            carry = substep(carry)
        for k in range(3):
            X[k] = carry[k]
            G[k] = carry[4 + k]

    for k, f in enumerate((4, 5, 7)):
        D[k] = roll(X[f], 1, 1)
        F[k] = roll(G[f], 1, 1)
    masks = X[3, own, 0:ny], X[4, own, 0:ny]
    h_ref, u_ref, v_ref = thick, vel_u, vel_v
    n_h, n_u, n_v = mid_h, mid_u, mid_v
    for step in range(STEPS - 1):
        substeps()
        pack_rows(step + 1, 0, 3)
        tile = send_tile(step + 1, 3)
        lead = (far_west, even)
        each(*lead, lambda c: start_all(c[:-1]), tile)
        pack_edges(step + 1, 3)
        each(*lead, lambda c: c[-1].start(), tile)
        tile[2].start()
        start_folds(tile[3], lambda zz: zz != z)
        for _, near_copy, zz in tile[3]:
            pl.when(jnp.logical_and(top, zz == z))(near_copy.start)
        each(even, far_west, start_all, tile)
        wait_layers(out)
        close_step(step, h_ref, v_ref, n_h, n_u, n_v)
        h_ref, u_ref, v_ref = n_h, n_u, n_v
        n_h, n_u, n_v = o_h, o_u, o_v
        out = send_layers(step + 1, h_ref, u_ref, v_ref)
        start_layers(out, False)
        layer_trial(h_ref, u_ref, v_ref, n_h, n_u, n_v, sums, False)
        take_tile(step + 1, 3, *tile)
    substeps()
    for f in range(3):
        flat[f] = X[f, own, 0:ny]
    wait_layers(out)
    close_step(STEPS - 1, h_ref, v_ref, n_h, n_u, n_v)


def body(zonal_devices, merid_devices, *args):
    thickness = args[3]
    layers, nx, ny = thickness.shape
    up = tile_up(layers)
    f32 = jnp.float32
    vmem = pl.BlockSpec(memory_space=pltpu.VMEM)
    far = pl.BlockSpec(memory_space=pltpu.HBM)
    hbm = pl.BlockSpec(memory_space=pl.ANY)
    rows = nx + 2 * PAD
    west, east = tile_up(sum(WEST)), tile_up(sum(EAST))
    plane = jax.ShapeDtypeStruct((nx, ny), f32)
    solid = jax.ShapeDtypeStruct((layers, nx, ny), f32)
    kept = [(3, nx, ny), (layers, nx, ny), (layers, nx, ny), (layers, nx, ny)]
    room = sum(math.prod(shape) for shape in kept)
    args = list(args)
    args[7] = args[7].T
    between = pl.pallas_call(
        functools.partial(kernel, zonal_devices, merid_devices),
        out_shape=[pltpu.VMEM(shape, f32) for shape in kept],
        in_specs=[far] * 10,
        out_specs=[vmem] * len(kept),
        scratch_shapes=[
            pltpu.VMEM((layers, nx, ny), f32),
            pltpu.VMEM((layers, nx, ny), f32),
            pltpu.VMEM((layers, nx, ny), f32),
            pltpu.VMEM((2, nx, ny), jnp.int32),
            pltpu.SMEM(args[7].shape, jnp.int32),
            pltpu.SMEM(args[8].shape, f32),
            pltpu.VMEM((layers, nx, ny), f32),
            pltpu.VMEM((layers, nx, ny), f32),
            pltpu.VMEM((layers, nx, ny), f32),
            pltpu.VMEM((2, nx, ny), f32),
            pltpu.VMEM((4, nx, ny), f32),
            pltpu.VMEM((2, nx, ny), f32),
            pltpu.VMEM((FIELDS, rows, ny + LANES), f32),
            pltpu.VMEM((FIELDS, rows, LANES), f32),
            pltpu.VMEM((3, rows, ny + LANES), f32),
            pltpu.VMEM((3, rows, LANES), f32),
            pltpu.VMEM((2, rows, ny + LANES), f32),
            pltpu.VMEM((2, rows, LANES), f32),
            pltpu.VMEM((STEPS, west, ny), f32),
            pltpu.VMEM((STEPS, west, ny), f32),
            pltpu.VMEM((STEPS, east, ny), f32),
            pltpu.VMEM((STEPS, east, ny), f32),
            pltpu.VMEM((STEPS, 3, nx, LANES), f32),
            pltpu.VMEM((STEPS, rows, LANES), f32),
            pltpu.VMEM((STEPS, rows, LANES), f32),
            pltpu.VMEM((STEPS, 2 * up, ny), f32),
            pltpu.VMEM((STEPS, up, ny), f32),
            pltpu.VMEM((STEPS, 2 * up, ny), f32),
            pltpu.VMEM((STEPS, up, ny), f32),
            pltpu.VMEM((STEPS, 3, nx, LANES), f32),
            pltpu.VMEM((STEPS, 2, nx, LANES), f32),
            pltpu.SemaphoreType.DMA((10,)),
            pltpu.SemaphoreType.DMA((STEPS, 10)),
            pltpu.SemaphoreType.DMA((STEPS, 10)),
            pltpu.SemaphoreType.DMA((STEPS, 4)),
            pltpu.SemaphoreType.DMA((STEPS, 4)),
            pltpu.SemaphoreType.REGULAR((2,)),
        ],
        compiler_params=pltpu.CompilerParams(
            collective_id=0, has_side_effects=True, vmem_limit_bytes=VMEM_BYTES - 4 * room - SPARE
        ),
        name="ocean",
    )(*args)
    return pl.pallas_call(
        last_kernel,
        out_shape=(plane, plane, plane, solid, solid, solid),
        in_specs=[vmem] * len(kept),
        out_specs=[hbm] * 6,
        scratch_shapes=[pltpu.SemaphoreType.DMA((3 + 3 * PIECES,))],
        compiler_params=pltpu.CompilerParams(vmem_limit_bytes=24 * 1024 * 1024),
        name="last",
    )(*between)


def solution(mesh):
    field = P(("members", "zonal"), "merid")
    solid = P(None, ("members", "zonal"), "merid")
    fixed = P(None, "zonal", "merid")
    return jax.shard_map(
        functools.partial(body, mesh.shape["zonal"], mesh.shape["merid"]),
        mesh=mesh,
        in_specs=(
            field, field, field, solid, solid, solid, fixed, P("members", None), P("members"), fixed,
        ),
        out_specs=(field, field, field, solid, solid, solid),
        check_vma=False,
    )
```

profile of v0, /device:TPU:0, one launch (start us, length us, event | category | flops | bytes accessed | tf_op | source)
XLA Modules:
  0.0 22.0 jit_solution(2495586060639952851)
XLA Ops:
  0.6 20.2 %ocean.1 = (f32[3,16,512]{2,1,0:T(8,128)S(1)}, f32[14,16,512]{2,1,0:T(8,128)S(1)}, f32[14,16,512]{2,1,0:T(8,128)S(1)}, f32[14,16,512]{2,1,0:T(8,128)S(1)}) custom-call(f32[16,512]{1,0:T(8,128)} %height_any.1, f32[16,512]{1,0:T(8,128)} %trans_u_any.1, f32[16,512]{1,0:T(8,128)} %trans_v_any.1, f32[14,16,512]{2,1,0:T(8,128)} %thick_any.1, ...), custom_call_target="tpu_custom_call" | custom-call | tf_op jit(solution)/shard_map/ocean/pallas_call | solution.py:605
  20.8 1.2 %last.1 = (f32[16,512]{1,0:T(8,128)}, f32[16,512]{1,0:T(8,128)}, f32[16,512]{1,0:T(8,128)}, f32[14,16,512]{2,1,0:T(8,128)}, f32[14,16,512]{2,1,0:T(8,128)}, /*index=5*/f32[14,16,512]{2,1,0:T(8,128)}) custom-call(f32[3,16,512]{2,1,0:T(8,128)S(1)} %get-tuple-element.10.flat, f32[14,16,512]{2,1,0:T(8,128)S(1)} %get-tuple-element.11.n_h, ...), custom_call_target="tpu_custom_call" | custom-call | tf_op jit(solution)/shard_map/last/pallas_call | solution.py:654
where the time goes:
time: 22.2 us; the launch traced here: 22 us
  Pallas kernels  21.4 us (96%)
  between operations  0.64 us (3%)
    pallas_call x1, Pallas kernels, body(): pl.pallas_call(functools.partial(kernel, zonal_devices, merid_devices), o...  20.2 us
    pallas_call x1, Pallas kernels, body(): pl.pallas_call(last_kernel, out_shape=(plane, plane, plane, solid, solid,...  1.18 us

commit v1 on v0

--- a/solution.py
+++ b/solution.py
@@ -26,7 +26,6 @@
 EAST = (NSUB, NSUB, NSUB) + (NSUB - 1,) * 5
 ORDER = (0, 1, 2, 3, 4, 6, 7, 5)
 CUT = 32
-PIECES = 2
 MESH = pl.DeviceIdType.MESH
 
 
@@ -42,6 +41,14 @@
     part = seed * index * (1.0 / total)
     angle = (2.0 * math.pi) * (part - jnp.floor(part))
     return jnp.cos(angle), jnp.sin(angle)
+
+
+def lines(ref):
+    return math.prod(ref.shape) // LANES
+
+
+def drain(ref, sem):
+    pltpu.make_async_copy(ref, ref, sem).wait()
 
 
 def tile_up(count):
@@ -142,17 +149,13 @@
 
 
 def last_kernel(flat, n_h, n_u, n_v, o_eta, o_bu, o_bv, o_h, o_u, o_v, sems):
-    layers = n_h.shape[0]
-    moves = [(flat.at[k], o) for k, o in enumerate((o_eta, o_bu, o_bv))]
-    cut = layers // PIECES
-    for n, o in ((n_h, o_h), (n_u, o_u), (n_v, o_v)):
-        for p in range(PIECES):
-            part = slice(p * cut, layers if p == PIECES - 1 else (p + 1) * cut)
-            moves.append((n.at[part], o.at[part]))
-    copies = [pltpu.make_async_copy(src, dst, sems.at[k]) for k, (src, dst) in enumerate(moves)]
+    moves = [(flat.at[k], o, 0) for k, o in enumerate((o_eta, o_bu, o_bv))]
+    moves += [(n_h, o_h, 1), (n_u, o_u, 2), (n_v, o_v, 3)]
+    copies = [pltpu.make_async_copy(src, dst, sems.at[k]) for src, dst, k in moves]
     for copy in copies:
         copy.start()
-    for copy in copies:
+    drain(flat, sems.at[0])
+    for copy in copies[3:]:
         copy.wait()
 
 
@@ -174,8 +177,7 @@
     o_u,
     o_v,
     thick,
-    vel_u,
-    vel_v,
+    vel,
     faces,
     seeds,
     scale,
@@ -204,10 +206,10 @@
     lay_recv_e,
     lay_pack_send,
     lay_pack_recv,
+    blank,
     load_sem,
     send_sem,
     recv_sem,
-    lay_send_sem,
     lay_recv_sem,
     late_sem,
 ):
@@ -256,12 +258,14 @@
         (trans_v_any, X.at[2, own, 0:ny]),
         (base_any, X.at[6:8, own, 0:ny]),
         (thick_any, thick),
-        (vel_u_any, vel_u),
-        (vel_v_any, vel_v),
+        (vel_u_any, vel.at[0]),
+        (vel_v_any, vel.at[1]),
         (seeds_any, seeds),
         (scale_any, scale),
     )
-    loads = [pltpu.make_async_copy(src, dst, load_sem.at[k]) for k, (src, dst) in enumerate(moves)]
+    group = (0, 0, 0, 0, 0, 1, 2, 2, 3, 4)
+    vel_u, vel_v = vel.at[0], vel.at[1]
+    loads = [pltpu.make_async_copy(src, dst, load_sem.at[k]) for k, (src, dst) in zip(group, moves)]
     for load in loads:
         load.start()
 
@@ -281,11 +285,9 @@
         def _():
             greet(late_sem.at[1], zz, m)
 
-    loads[0].wait()
+    drain(blank.at[0 : sum(lines(dst) for _, dst in moves[:5])], load_sem.at[0])
     X[3, own, 0:ny] = faces[0].astype(jnp.float32)
     X[4, own, 0:ny] = faces[1].astype(jnp.float32)
-    for load in loads[1:5]:
-        load.wait()
 
     def pack_rows(step, start, stop):
         west = sum(WEST[f] for f in ORDER[:start])
@@ -296,7 +298,7 @@
             west += WEST[f]
             east += EAST[f]
 
-    def pack_edges(step, fields):
+    def pack_edges(step, fields, between=lambda: None):
         inner = jnp.zeros((nx, LANES), jnp.float32)
         crest = jnp.zeros((nx, LANES), jnp.float32)
         for f in range(fields):
@@ -306,17 +308,21 @@
             crest = jnp.where(here, high, crest)
             inner = jnp.where(here, jnp.where(bottom, high, low), inner)
         pack_send[step, 0] = inner
+        between()
         pack_send[step, 2] = crest
         for r in range(nx):
             pack_send[step, 1, r : r + 1, :] = pack_send[step, 2, nx - 1 - r : nx - r, :]
 
+    leaving = {}
+
     def send_tile(step, fields):
         def send(src, dst, k, zz, mm):
+            leaving[k] = leaving.get(k, 0) + lines(src)
             return pltpu.make_async_remote_copy(
                 src_ref=src,
                 dst_ref=dst,
-                send_sem=send_sem.at[step, k],
-                recv_sem=recv_sem.at[step, k],
+                send_sem=send_sem.at[k],
+                recv_sem=recv_sem.at[step],
                 device_id={"zonal": zz, "merid": mm},
                 device_id_type=MESH,
             )
@@ -324,21 +330,21 @@
         def rows_of(src, dst, k, zz, count):
             cuts = [0, CUT, count] if count > CUT else [0, count]
             parts = [slice(low, high) for low, high in zip(cuts[:-1], cuts[1:])]
-            return [send(src.at[step, p], dst.at[step, p], k + 2 * n, zz, m) for n, p in enumerate(parts)]
+            return [send(src.at[step, p], dst.at[step, p], 0 if n else k, zz, m) for n, p in enumerate(parts)]
 
         tail, whole, start = slice(nx - PAD, nx), slice(0, nx), slice(0, PAD)
         places = (slice(0, PAD), own, slice(PAD + nx, rows))
         inner = lambda s, part: (pack_send.at[step, 0, part], inner_recv.at[step, places[s]])
         west = rows_of(west_send, west_recv, 0, right, tile_up(sum(WEST[:fields])))
-        east = rows_of(east_send, east_recv, 1, left, tile_up(sum(EAST[:fields])))
-        west.append(send(*inner(0, tail), 6, right, other))
-        east.append(send(*inner(2, start), 4, left, other))
-        across = send(*inner(1, whole), 5, z, other)
+        east = rows_of(east_send, east_recv, int(step == 0), left, tile_up(sum(EAST[:fields])))
+        west.append(send(*inner(0, tail), 0, right, other))
+        east.append(send(*inner(2, start), 0, left, other))
+        across = send(*inner(1, whole), 0, z, other)
         folds = []
         for s, part, zz in ((2, start, mirror_w), (1, whole, mirror), (0, tail, mirror_e)):
             src, dst = pack_send.at[step, 1, part], fold_recv.at[step, places[s]]
-            near = pltpu.make_async_copy(src, dst, recv_sem.at[step, 7 + s])
-            folds.append((send(src, dst, 7 + s, zz, m), near, zz))
+            near = pltpu.make_async_copy(src, dst, recv_sem.at[step])
+            folds.append((send(src, dst, 2 + s, zz, m), near, zz))
         return west, east, across, folds
 
     even = lax.rem(z, 2) == 0
@@ -357,18 +363,13 @@
         for far_copy, _, zz in folds:
             pl.when(jnp.logical_and(top, chosen(zz)))(far_copy.start)
 
-    def take_tile(step, fields, west_copies, east_copies, across, folds):
-        for copy in west_copies + east_copies + [across]:
-            copy.wait()
-        for far_copy, near_copy, zz in folds:
-
-            @pl.when(jnp.logical_and(top, zz != z))
-            def _():
-                far_copy.wait()
-
-            @pl.when(jnp.logical_and(top, zz == z))
-            def _():
-                near_copy.wait()
+    def take(sem, always, at_top):
+        pl.when(bottom)(lambda: drain(blank.at[0:always], sem))
+        pl.when(top)(lambda: drain(blank.at[0 : always + at_top], sem))
+
+    def take_tile(step, fields):
+        count = tile_up(sum(WEST[f] for f in ORDER[:fields])) + tile_up(sum(EAST[f] for f in ORDER[:fields]))
+        take(recv_sem.at[step], count * ny // LANES + rows, rows)
 
         west = east = 0
         for f in ORDER[:fields]:
@@ -384,7 +385,7 @@
             G[f] = roll(fold_recv[step], LANES - SLOT * (f + 1), 1)
 
     pack_rows(0, 0, FIELDS - 1)
-    tile = send_tile(0, FIELDS)
+    tile = tile_0 = send_tile(0, FIELDS)
     lead = (jnp.logical_or(far_west, first_z), far_east)
     each(*lead, lambda c: c[0].start(), tile)
     loads[5].wait()
@@ -402,21 +403,22 @@
         pl.when(jnp.logical_and(top, zz == z))(near_copy.start)
 
     def lay_copies(step):
-        def one(src, dst, k, zz, mm):
+        def one(src, dst, zz, mm, k=0):
+            leaving[k] = leaving.get(k, 0) + lines(src)
             return pltpu.make_async_remote_copy(
                 src_ref=src,
                 dst_ref=dst,
-                send_sem=lay_send_sem.at[step, k],
-                recv_sem=lay_recv_sem.at[step, k],
+                send_sem=send_sem.at[k],
+                recv_sem=lay_recv_sem.at[step],
                 device_id={"zonal": zz, "merid": mm},
                 device_id_type=MESH,
             )
 
         return [
-            one(lay_send_r.at[step], lay_recv_w.at[step], 0, right, m),
-            one(lay_send_l.at[step], lay_recv_e.at[step], 1, left, m),
-            one(lay_pack_send.at[step, 0], lay_pack_recv.at[step, 0], 2, z, other),
-            one(lay_pack_send.at[step, 1], lay_pack_recv.at[step, 1], 3, mirror, m),
+            one(lay_send_r.at[step], lay_recv_w.at[step], right, m),
+            one(lay_send_l.at[step], lay_recv_e.at[step], left, m),
+            one(lay_pack_send.at[step, 0], lay_pack_recv.at[step, 0], z, other),
+            one(lay_pack_send.at[step, 1], lay_pack_recv.at[step, 1], mirror, m, 3),
         ]
 
     above = lay_send_r.shape[1] // 2
@@ -449,15 +451,17 @@
         if first:
             pl.when(first_z)(out[0].start)
 
-    def wait_layers(out):
-        for copy in out[:3]:
-            copy.wait()
-
-        @pl.when(top)
-        def _():
-            out[3].wait()
-
-    for load in loads[6:]:
+    def wait_layers(step):
+        take(lay_recv_sem.at[step], lines(lay_recv_w.at[step]) + lines(lay_recv_e.at[step]) + nx, nx)
+
+    def wait_sent():
+        drain(blank.at[0 : leaving[0]], send_sem.at[0])
+        pl.when(jnp.logical_not(first_z))(tile_0[1][0].wait_send)
+        for k, zz in zip((4, 3, 2), mirrors):
+            pl.when(jnp.logical_and(top, zz != z))(lambda k=k: drain(blank.at[0 : leaving[k]], send_sem.at[k]))
+
+    drain(vel, load_sem.at[2])
+    for load in loads[8:]:
         load.wait()
     out = send_layers(0, thick, vel_u, vel_v)
 
@@ -504,10 +508,14 @@
         pl.semaphore_wait(late_sem.at[1], upper)
 
     start_folds(tile[3], lambda zz: zz > z)
-    pl.when(first_z)(out[1].start)
     pl.when(jnp.logical_and(top, mirror > z))(out[3].start)
 
-    take_tile(0, FIELDS, *tile)
+    @pl.when(first_z)
+    def _():
+        tile[1][0].wait_send()
+        out[1].start()
+
+    take_tile(0, FIELDS)
     for k in range(2):
         X[6 + k] = STRESS_SCALE * (X[6 + k] + wind_own[k])
         G[6 + k] = STRESS_SCALE * (G[6 + k] + wind_far[k])
@@ -564,26 +572,30 @@
         tile = send_tile(step + 1, 3)
         lead = (far_west, even)
         each(*lead, lambda c: start_all(c[:-1]), tile)
-        pack_edges(step + 1, 3)
-        each(*lead, lambda c: c[-1].start(), tile)
-        tile[2].start()
+
+        def inner_ready():
+            each(*lead, lambda c: c[-1].start(), tile)
+            tile[2].start()
+
+        pack_edges(step + 1, 3, inner_ready)
         start_folds(tile[3], lambda zz: zz != z)
         for _, near_copy, zz in tile[3]:
             pl.when(jnp.logical_and(top, zz == z))(near_copy.start)
         each(even, far_west, start_all, tile)
-        wait_layers(out)
+        wait_layers(step)
         close_step(step, h_ref, v_ref, n_h, n_u, n_v)
         h_ref, u_ref, v_ref = n_h, n_u, n_v
         n_h, n_u, n_v = o_h, o_u, o_v
         out = send_layers(step + 1, h_ref, u_ref, v_ref)
         start_layers(out, False)
         layer_trial(h_ref, u_ref, v_ref, n_h, n_u, n_v, sums, False)
-        take_tile(step + 1, 3, *tile)
+        take_tile(step + 1, 3)
     substeps()
     for f in range(3):
         flat[f] = X[f, own, 0:ny]
-    wait_layers(out)
+    wait_layers(STEPS - 1)
     close_step(STEPS - 1, h_ref, v_ref, n_h, n_u, n_v)
+    wait_sent()
 
 
 def body(zonal_devices, merid_devices, *args):
@@ -609,8 +621,7 @@
         out_specs=[vmem] * len(kept),
         scratch_shapes=[
             pltpu.VMEM((layers, nx, ny), f32),
-            pltpu.VMEM((layers, nx, ny), f32),
-            pltpu.VMEM((layers, nx, ny), f32),
+            pltpu.VMEM((2, layers, nx, ny), f32),
             pltpu.VMEM((2, nx, ny), jnp.int32),
             pltpu.SMEM(args[7].shape, jnp.int32),
             pltpu.SMEM(args[8].shape, f32),
@@ -639,11 +650,11 @@
             pltpu.VMEM((STEPS, up, ny), f32),
             pltpu.VMEM((STEPS, 3, nx, LANES), f32),
             pltpu.VMEM((STEPS, 2, nx, LANES), f32),
-            pltpu.SemaphoreType.DMA((10,)),
-            pltpu.SemaphoreType.DMA((STEPS, 10)),
-            pltpu.SemaphoreType.DMA((STEPS, 10)),
-            pltpu.SemaphoreType.DMA((STEPS, 4)),
-            pltpu.SemaphoreType.DMA((STEPS, 4)),
+            pltpu.VMEM((4 * (west + east) * ny // LANES, LANES), f32),
+            pltpu.SemaphoreType.DMA((5,)),
+            pltpu.SemaphoreType.DMA((5,)),
+            pltpu.SemaphoreType.DMA((STEPS,)),
+            pltpu.SemaphoreType.DMA((STEPS,)),
             pltpu.SemaphoreType.REGULAR((2,)),
         ],
         compiler_params=pltpu.CompilerParams(
@@ -656,7 +667,7 @@
         out_shape=(plane, plane, plane, solid, solid, solid),
         in_specs=[vmem] * len(kept),
         out_specs=[hbm] * 6,
-        scratch_shapes=[pltpu.SemaphoreType.DMA((3 + 3 * PIECES,))],
+        scratch_shapes=[pltpu.SemaphoreType.DMA((4,))],
         compiler_params=pltpu.CompilerParams(vmem_limit_bytes=24 * 1024 * 1024),
         name="last",
     )(*between)

time: 22.2 us -> 21.6 us (0.973)
  Pallas kernels: 21.4 us -> 20.8 us
    pallas_call x1, Pallas kernels: 20.2 us -> 19.7 us  [body(): pl.pallas_call(functools.partial(kernel, zonal_devices, merid_devices), o...]
where the time goes in v1:
time: 21.6 us; the launch traced here: 21.5 us
  Pallas kernels  20.8 us (96%)
  between operations  0.64 us (3%)
    pallas_call x1, Pallas kernels, body(): pl.pallas_call(functools.partial(kernel, zonal_devices, merid_devices), o...  19.7 us
    pallas_call x1, Pallas kernels, body(): pl.pallas_call(last_kernel, out_shape=(plane, plane, plane, solid, solid,...  1.14 us

profile of v1, /device:TPU:0, one launch (start us, length us, event | category | flops | bytes accessed | tf_op | source)
XLA Modules:
  0.0 21.5 jit_solution(12563053280008215325)
XLA Ops:
  0.6 19.7 %ocean.1 = (f32[3,16,512]{2,1,0:T(8,128)S(1)}, f32[14,16,512]{2,1,0:T(8,128)S(1)}, f32[14,16,512]{2,1,0:T(8,128)S(1)}, f32[14,16,512]{2,1,0:T(8,128)S(1)}) custom-call(f32[16,512]{1,0:T(8,128)} %height_any.1, f32[16,512]{1,0:T(8,128)} %trans_u_any.1, f32[16,512]{1,0:T(8,128)} %trans_v_any.1, f32[14,16,512]{2,1,0:T(8,128)} %thick_any.1, ...), custom_call_target="tpu_custom_call" | custom-call | tf_op jit(solution)/shard_map/ocean/pallas_call | solution.py:617
  20.3 1.1 %last.1 = (f32[16,512]{1,0:T(8,128)}, f32[16,512]{1,0:T(8,128)}, f32[16,512]{1,0:T(8,128)}, f32[14,16,512]{2,1,0:T(8,128)}, f32[14,16,512]{2,1,0:T(8,128)}, /*index=5*/f32[14,16,512]{2,1,0:T(8,128)}) custom-call(f32[3,16,512]{2,1,0:T(8,128)S(1)} %get-tuple-element.10.flat, f32[14,16,512]{2,1,0:T(8,128)S(1)} %get-tuple-element.11.n_h, ...), custom_call_target="tpu_custom_call" | custom-call | tf_op jit(solution)/shard_map/last/pallas_call | solution.py:665

commit v2 on v1

--- a/solution.py
+++ b/solution.py
@@ -232,6 +232,7 @@
 
     barrier = pltpu.get_barrier_semaphore()
     first_z, last_z = z == 0, z == Z - 1
+    late_left = jnp.logical_or(first_z, last_z)
     mirrors = (mirror_w, mirror, mirror_e)
 
     def greet(sem, zz, mm):
@@ -240,10 +241,7 @@
     greet(barrier, z, other)
     for mm in (m, other):
         greet(barrier, left, mm)
-
-        @pl.when(jnp.logical_not(last_z))
-        def _():
-            greet(barrier, right, mm)
+        pl.when(z < Z - 2)(lambda mm=mm: greet(barrier, right, mm))
 
     for zz in mirrors:
 
@@ -269,12 +267,12 @@
     for load in loads:
         load.start()
 
-    near = 3 + jnp.where(first_z, 0, 2)
+    near = 3 + jnp.where(jnp.logical_or(first_z, last_z), 0, 2)
     lower = sum((zz < z).astype(jnp.int32) for zz in mirrors)
     upper = sum((zz > z).astype(jnp.int32) for zz in mirrors)
     pl.semaphore_wait(barrier, near + jnp.where(top, lower, 0))
 
-    @pl.when(last_z)
+    @pl.when(z >= Z - 2)
     def _():
         for mm in (m, other):
             greet(late_sem.at[0], right, mm)
@@ -330,7 +328,7 @@
         def rows_of(src, dst, k, zz, count):
             cuts = [0, CUT, count] if count > CUT else [0, count]
             parts = [slice(low, high) for low, high in zip(cuts[:-1], cuts[1:])]
-            return [send(src.at[step, p], dst.at[step, p], 0 if n else k, zz, m) for n, p in enumerate(parts)]
+            return [send(src.at[step, p], dst.at[step, p], k, zz, m) for p in parts]
 
         tail, whole, start = slice(nx - PAD, nx), slice(0, nx), slice(0, PAD)
         places = (slice(0, PAD), own, slice(PAD + nx, rows))
@@ -338,7 +336,7 @@
         west = rows_of(west_send, west_recv, 0, right, tile_up(sum(WEST[:fields])))
         east = rows_of(east_send, east_recv, int(step == 0), left, tile_up(sum(EAST[:fields])))
         west.append(send(*inner(0, tail), 0, right, other))
-        east.append(send(*inner(2, start), 0, left, other))
+        east.append(send(*inner(2, start), int(step == 0), left, other))
         across = send(*inner(1, whole), 0, z, other)
         folds = []
         for s, part, zz in ((2, start, mirror_w), (1, whole, mirror), (0, tail, mirror_e)):
@@ -396,7 +394,7 @@
     pack_rows(0, FIELDS - 1, FIELDS)
     pack_edges(0, FIELDS)
     each(*lead, lambda c: start_all(c[1:]), tile)
-    each(far_east, far_west, start_all, tile)
+    each(far_east, jnp.logical_and(far_west, jnp.logical_not(last_z)), start_all, tile)
     tile[2].start()
     start_folds(tile[3], lambda zz: zz < z)
     for _, near_copy, zz in tile[3]:
@@ -444,19 +442,18 @@
 
     def start_layers(out, first):
         out[2].start()
-        late_left, late_fold = (first_z, mirror > z) if first else (False, False)
+        hold, late_fold = (late_left, mirror > z) if first else (False, False)
         pl.when(jnp.logical_and(top, jnp.logical_not(late_fold)))(out[3].start)
-        pl.when(far_west)(lambda: start_all(out[:2]))
-        pl.when(jnp.logical_and(even, jnp.logical_not(late_left)))(lambda: start_all(out[1::-1]))
-        if first:
-            pl.when(first_z)(out[0].start)
+        pl.when(far_west)(out[0].start)
+        pl.when(jnp.logical_not(hold))(out[1].start)
+        pl.when(jnp.logical_not(far_west))(out[0].start)
 
     def wait_layers(step):
         take(lay_recv_sem.at[step], lines(lay_recv_w.at[step]) + lines(lay_recv_e.at[step]) + nx, nx)
 
     def wait_sent():
         drain(blank.at[0 : leaving[0]], send_sem.at[0])
-        pl.when(jnp.logical_not(first_z))(tile_0[1][0].wait_send)
+        pl.when(jnp.logical_not(first_z))(lambda: drain(blank.at[0 : leaving[1]], send_sem.at[1]))
         for k, zz in zip((4, 3, 2), mirrors):
             pl.when(jnp.logical_and(top, zz != z))(lambda k=k: drain(blank.at[0 : leaving[k]], send_sem.at[k]))
 
@@ -497,7 +494,7 @@
 
     layer_trial(thick, vel_u, vel_v, mid_h, mid_u, mid_v, sums, True)
 
-    @pl.when(first_z)
+    @pl.when(late_left)
     def _():
         pl.semaphore_wait(late_sem.at[0], 2)
         start_all(tile[1])
@@ -512,8 +509,9 @@
 
     @pl.when(first_z)
     def _():
-        tile[1][0].wait_send()
-        out[1].start()
+        drain(blank.at[0 : leaving[1]], send_sem.at[1])
+
+    pl.when(late_left)(out[1].start)
 
     take_tile(0, FIELDS)
     for k in range(2):
@@ -550,15 +548,14 @@
         mean[1] = mean[1] + bv[own, 0:ny]
         return eta, bu, bv, south_v, g_eta, g_bu, g_bv, g_south_v
 
-    def substeps():
+    def substeps(out):
         mean[...] = jnp.zeros((2, nx, ny), jnp.float32)
         bv, g_bv = X[2], G[2]
         carry = X[0], X[1], bv, jnp.where(wall, 0.0, roll(bv, 1, 1)), G[0], G[1], g_bv, roll(g_bv, 1, 1)
         for _ in range(NSUB):
             carry = substep(carry)
         for k in range(3):
-            X[k] = carry[k]
-            G[k] = carry[4 + k]
+            out[k, ...] = carry[k][own, 0:ny]
 
     for k, f in enumerate((4, 5, 7)):
         D[k] = roll(X[f], 1, 1)
@@ -567,7 +564,7 @@
     h_ref, u_ref, v_ref = thick, vel_u, vel_v
     n_h, n_u, n_v = mid_h, mid_u, mid_v
     for step in range(STEPS - 1):
-        substeps()
+        substeps(X.at[0:3, own, 0:ny])
         pack_rows(step + 1, 0, 3)
         tile = send_tile(step + 1, 3)
         lead = (far_west, even)
@@ -590,9 +587,7 @@
         start_layers(out, False)
         layer_trial(h_ref, u_ref, v_ref, n_h, n_u, n_v, sums, False)
         take_tile(step + 1, 3)
-    substeps()
-    for f in range(3):
-        flat[f] = X[f, own, 0:ny]
+    substeps(flat)
     wait_layers(STEPS - 1)
     close_step(STEPS - 1, h_ref, v_ref, n_h, n_u, n_v)
     wait_sent()

time: 21.6 us -> 21 us (0.972)
  Pallas kernels: 20.8 us -> 20.2 us
    pallas_call x1, Pallas kernels: 19.7 us -> 19.1 us  [body(): pl.pallas_call(functools.partial(kernel, zonal_devices, merid_devices), o...]
where the time goes in v2:
time: 21 us; the launch traced here: 20.9 us
  Pallas kernels  20.2 us (96%)
  between operations  0.64 us (3%)
    pallas_call x1, Pallas kernels, body(): pl.pallas_call(functools.partial(kernel, zonal_devices, merid_devices), o...  19.1 us
    pallas_call x1, Pallas kernels, body(): pl.pallas_call(last_kernel, out_shape=(plane, plane, plane, solid, solid,...  1.14 us

profile of v2, /device:TPU:0, one launch (start us, length us, event | category | flops | bytes accessed | tf_op | source)
XLA Modules:
  0.0 20.9 jit_solution(11490674390750311646)
XLA Ops:
  0.6 19.1 %ocean.1 = (f32[3,16,512]{2,1,0:T(8,128)S(1)}, f32[14,16,512]{2,1,0:T(8,128)S(1)}, f32[14,16,512]{2,1,0:T(8,128)S(1)}, f32[14,16,512]{2,1,0:T(8,128)S(1)}) custom-call(f32[16,512]{1,0:T(8,128)} %height_any.1, f32[16,512]{1,0:T(8,128)} %trans_u_any.1, f32[16,512]{1,0:T(8,128)} %trans_v_any.1, f32[14,16,512]{2,1,0:T(8,128)} %thick_any.1, ...), custom_call_target="tpu_custom_call" | custom-call | tf_op jit(solution)/shard_map/ocean/pallas_call | solution.py:612
  19.7 1.1 %last.1 = (f32[16,512]{1,0:T(8,128)}, f32[16,512]{1,0:T(8,128)}, f32[16,512]{1,0:T(8,128)}, f32[14,16,512]{2,1,0:T(8,128)}, f32[14,16,512]{2,1,0:T(8,128)}, /*index=5*/f32[14,16,512]{2,1,0:T(8,128)}) custom-call(f32[3,16,512]{2,1,0:T(8,128)S(1)} %get-tuple-element.10.flat, f32[14,16,512]{2,1,0:T(8,128)S(1)} %get-tuple-element.11.n_h, ...), custom_call_target="tpu_custom_call" | custom-call | tf_op jit(solution)/shard_map/last/pallas_call | solution.py:660

commit v3 on v2

--- a/solution.py
+++ b/solution.py
@@ -88,7 +88,18 @@
         sums[3] = deep_v
 
 
-def layer_edges(h_ref, v_ref, own_r, own_l, recv_w, recv_e, packs, o_h, o_u, o_v, sums, top, deep):
+def layer_close(o_u, o_v, sums, mean, masks, depth, deep):
+    if deep:
+        depth[0] = 1.0 / sums[2]
+        depth[1] = 1.0 / sums[3]
+    for k, out in enumerate((o_u, o_v)):
+        fix = (mean[k] * (1.0 / NSUB) - sums[k]) * depth[k]
+        mask = masks[k]
+        for l in range(out.shape[0]):
+            out[l] = mask * (out[l] + fix)
+
+
+def layer_edges(h_ref, v_ref, own_r, own_l, recv_w, recv_e, packs, o_h, o_u, o_v, mean, masks, depth, top, deep):
     layers, nx, ny = h_ref.shape
     up = own_l.shape[0]
     layer = iota((up, ny), 0)
@@ -104,11 +115,12 @@
     outflow = FLUX_STEP * (u_last * hu)
     inflow = FLUX_STEP * (u_w * ((h_w + h_first) * 0.5))
     whole = lambda a: jnp.sum(jnp.where(layer < layers, a, 0.0), axis=0, keepdims=True)
-    sums[0, nx - 1 : nx, :] = whole(hu * trial)
     if deep:
-        sums[2, nx - 1 : nx, :] = whole(hu)
+        depth[0, nx - 1 : nx, :] = 1.0 / whole(hu)
+    fix = (mean[0, nx - 1 : nx, :] * (1.0 / NSUB) - whole(hu * trial)) * depth[0, nx - 1 : nx, :]
+    edge_u = masks[0][nx - 1 : nx, :] * (trial + fix)
     for l in range(layers):
-        o_u[l, nx - 1 : nx, :] = trial[l : l + 1]
+        o_u[l, nx - 1 : nx, :] = edge_u[l : l + 1]
         o_h[l, nx - 1 : nx, :] = o_h[l, nx - 1 : nx, :] - outflow[l : l + 1]
         o_h[l, 0:1, :] = o_h[l, 0:1, :] + inflow[l : l + 1]
 
@@ -119,33 +131,25 @@
     side = packs[0]
     cap = jnp.where(top, packs[1], side)
     press, total, deep_v = 0.0, 0.0, 0.0
+    trials = []
     for l in range(layers):
         h, v = h_ref[l, :, last:ny], v_ref[l, :, last:ny]
         h_north = roll(cap, LANES - 1 - l, 1)
         hv = (h + h_north) * 0.5
         press = press + (h_north - h)
-        trial = v - PRESS_COEF * press
-        total = total + hv * trial
+        trials.append(v - PRESS_COEF * press)
+        total = total + hv * trials[l]
         deep_v = deep_v + hv
-        o_v[l, :, last:ny] = jnp.where(at_end, trial, o_v[l, :, last:ny])
         o_h[l, :, last:ny] = o_h[l, :, last:ny] - jnp.where(at_end, FLUX_STEP * (v * hv), 0.0)
         h_south, v_south = roll(side, -l, 1), roll(side, -(layers + l), 1)
         inflow = FLUX_STEP * (v_south * ((h_south + h_ref[l, :, 0:LANES]) * 0.5))
         o_h[l, :, 0:LANES] = o_h[l, :, 0:LANES] + jnp.where(at_start, inflow, 0.0)
-    sums[1, :, last:ny] = jnp.where(at_end, total, sums[1, :, last:ny])
     if deep:
-        sums[3, :, last:ny] = jnp.where(at_end, deep_v, sums[3, :, last:ny])
-
-
-def layer_close(o_u, o_v, sums, mean, masks, depth, deep):
-    if deep:
-        depth[0] = 1.0 / sums[2]
-        depth[1] = 1.0 / sums[3]
-    for k, out in enumerate((o_u, o_v)):
-        fix = (mean[k] * (1.0 / NSUB) - sums[k]) * depth[k]
-        mask = masks[k]
-        for l in range(out.shape[0]):
-            out[l] = mask * (out[l] + fix)
+        depth[1, :, last:ny] = jnp.where(at_end, 1.0 / deep_v, depth[1, :, last:ny])
+    fix = (mean[1, :, last:ny] * (1.0 / NSUB) - total) * depth[1, :, last:ny]
+    for l in range(layers):
+        edge_v = masks[1][:, last:ny] * (trials[l] + fix)
+        o_v[l, :, last:ny] = jnp.where(at_end, edge_v, o_v[l, :, last:ny])
 
 
 def last_kernel(flat, n_h, n_u, n_v, o_eta, o_bu, o_bv, o_h, o_u, o_v, sems):
@@ -197,6 +201,8 @@
     west_recv,
     east_send,
     east_recv,
+    spare_send,
+    spare_recv,
     pack_send,
     inner_recv,
     fold_recv,
@@ -287,12 +293,20 @@
     X[3, own, 0:ny] = faces[0].astype(jnp.float32)
     X[4, own, 0:ny] = faces[1].astype(jnp.float32)
 
+    blocks = ny // LANES
+    full_east = sum(EAST) // 8 * 8
+
     def pack_rows(step, start, stop):
         west = sum(WEST[f] for f in ORDER[:start])
         east = sum(EAST[f] for f in ORDER[:start])
         for f in ORDER[start:stop]:
             west_send[step, west : west + WEST[f], :] = X[f, PAD + nx - WEST[f] : PAD + nx, 0:ny]
-            east_send[step, east : east + EAST[f], :] = X[f, PAD : PAD + EAST[f], 0:ny]
+            fits = EAST[f] if step else min(EAST[f], full_east - east)
+            east_send[step, east : east + fits, :] = X[f, PAD : PAD + fits, 0:ny]
+            for q in range(fits, EAST[f]):
+                for t in range(blocks):
+                    at = (q - fits) * blocks + t
+                    spare_send[at : at + 1, :] = X[f, PAD + q : PAD + q + 1, t * LANES : (t + 1) * LANES]
             west += WEST[f]
             east += EAST[f]
 
@@ -334,7 +348,9 @@
         places = (slice(0, PAD), own, slice(PAD + nx, rows))
         inner = lambda s, part: (pack_send.at[step, 0, part], inner_recv.at[step, places[s]])
         west = rows_of(west_send, west_recv, 0, right, tile_up(sum(WEST[:fields])))
-        east = rows_of(east_send, east_recv, int(step == 0), left, tile_up(sum(EAST[:fields])))
+        east = rows_of(east_send, east_recv, int(step == 0), left, tile_up(sum(EAST[:fields])) if step else full_east)
+        if not step:
+            east.append(send(spare_send, spare_recv, 1, left, m))
         west.append(send(*inner(0, tail), 0, right, other))
         east.append(send(*inner(2, start), int(step == 0), left, other))
         across = send(*inner(1, whole), 0, z, other)
@@ -366,13 +382,18 @@
         pl.when(top)(lambda: drain(blank.at[0 : always + at_top], sem))
 
     def take_tile(step, fields):
-        count = tile_up(sum(WEST[f] for f in ORDER[:fields])) + tile_up(sum(EAST[f] for f in ORDER[:fields]))
-        take(recv_sem.at[step], count * ny // LANES + rows, rows)
+        count = tile_up(sum(WEST[:fields])) + (tile_up(sum(EAST[:fields])) if step else full_east)
+        take(recv_sem.at[step], count * blocks + rows + (0 if step else lines(spare_recv)), rows)
 
         west = east = 0
         for f in ORDER[:fields]:
             X[f, PAD - WEST[f] : PAD, 0:ny] = west_recv[step, west : west + WEST[f], :]
-            X[f, PAD + nx : PAD + nx + EAST[f], 0:ny] = east_recv[step, east : east + EAST[f], :]
+            fits = EAST[f] if step else min(EAST[f], full_east - east)
+            X[f, PAD + nx : PAD + nx + fits, 0:ny] = east_recv[step, east : east + fits, :]
+            for q in range(fits, EAST[f]):
+                for t in range(blocks):
+                    at, row = (q - fits) * blocks + t, PAD + nx + q
+                    X[f, row : row + 1, t * LANES : (t + 1) * LANES] = spare_recv[at : at + 1, :]
             west += WEST[f]
             east += EAST[f]
         for f in range(fields):
@@ -514,57 +535,70 @@
     pl.when(late_left)(out[1].start)
 
     take_tile(0, FIELDS)
-    for k in range(2):
-        X[6 + k] = STRESS_SCALE * (X[6 + k] + wind_own[k])
-        G[6 + k] = STRESS_SCALE * (G[6 + k] + wind_far[k])
-
     lanes = iota((rows, width), 1)
     wall = jnp.logical_and(bottom, lanes == 0)
-    crown = jnp.logical_and(top, lanes == ny - 1)
+    crown = jnp.logical_and(top, iota((rows, LANES), 1) == LANES - 1)
     far_top = iota((rows, LANES), 1) == LANES - 1
+
+    def southern(bv, g_bv):
+        return jnp.where(wall, 0.0, roll(bv, 1, 1)), roll(g_bv, 1, 1)
+
+    for k in range(2):
+        mask, far_mask = X[3 + k], G[3 + k]
+        D[2 * k] = mask * X[5]
+        F[2 * k] = far_mask * G[5]
+        D[2 * k + 1] = mask * (STRESS_SCALE * (X[6 + k] + wind_own[k]))
+        F[2 * k + 1] = far_mask * (STRESS_SCALE * (G[6 + k] + wind_far[k]))
+    for k in range(2):
+        D[4 + k], F[4 + k] = southern(D[2 + k], F[2 + k])
 
     def close_step(step, h_ref, v_ref, n_h, n_u, n_v):
         layer_edges(
             h_ref, v_ref, lay_send_r.at[step], lay_send_l.at[step], lay_recv_w.at[step], lay_recv_e.at[step],
-            lay_pack_recv.at[step], n_h, n_u, n_v, sums, top, step == 0,
+            lay_pack_recv.at[step], n_h, n_u, n_v, mean, masks, depth, top, step == 0,
         )
-        layer_close(n_u, n_v, sums, mean, masks, depth, step == 0)
-
-    def substep(carry):
+
+    def substep(carry, masked):
         eta, bu, bv, south_v, g_eta, g_bu, g_bv, g_south_v = carry
         eta = eta - (bu - roll(bu, 1, 0) + bv - south_v)
         g_eta = g_eta - (g_bu - roll(g_bu, -1, 0) + g_bv - g_south_v)
+        if masked:
+            bu, bv, south_v, g_bu, g_bv, g_south_v = masked
         north, south = roll(eta, -1, 1), roll(eta, 1, 1)
-        north = jnp.where(crown, g_eta[:, LANES - 1 :], north)
+        brink = jnp.where(crown, g_eta[:, LANES - 1 :], north[:, last:ny])
+        north = jnp.concatenate([north[:, :last], brink, north[:, ny:]], axis=1)
         g_north = jnp.where(far_top, eta[:, ny - 1 : ny], roll(g_eta, -1, 1))
         g_south = roll(g_eta, 1, 1)
-        bu = X[3] * (bu - X[5] * (roll(eta, -1, 0) - eta) + X[6])
-        bv = X[4] * (bv - X[5] * (north - eta) + X[7])
-        south_v = jnp.where(wall, 0.0, D[0] * (south_v - D[1] * (eta - south) + D[2]))
-        g_bu = G[3] * (g_bu - G[5] * (roll(g_eta, 1, 0) - g_eta) + G[6])
-        g_bv = G[4] * (g_bv - G[5] * (g_north - g_eta) + G[7])
-        g_south_v = F[0] * (g_south_v - F[1] * (g_eta - g_south) + F[2])
+        bu = bu - D[0] * (roll(eta, -1, 0) - eta) + D[1]
+        bv = bv - D[2] * (north - eta) + D[3]
+        south_v = south_v - D[4] * (eta - south) + D[5]
+        g_bu = g_bu - F[0] * (roll(g_eta, 1, 0) - g_eta) + F[1]
+        g_bv = g_bv - F[2] * (g_north - g_eta) + F[3]
+        g_south_v = g_south_v - F[4] * (g_eta - g_south) + F[5]
         mean[0] = mean[0] + bu[own, 0:ny]
         mean[1] = mean[1] + bv[own, 0:ny]
         return eta, bu, bv, south_v, g_eta, g_bu, g_bv, g_south_v
 
-    def substeps(out):
+    def substeps(out, raw):
         mean[...] = jnp.zeros((2, nx, ny), jnp.float32)
-        bv, g_bv = X[2], G[2]
-        carry = X[0], X[1], bv, jnp.where(wall, 0.0, roll(bv, 1, 1)), G[0], G[1], g_bv, roll(g_bv, 1, 1)
-        for _ in range(NSUB):
-            carry = substep(carry)
+        bu, bv, g_bu, g_bv = X[1], X[2], G[1], G[2]
+        south_v, g_south_v = southern(bv, g_bv)
+        carry = X[0], bu, bv, south_v, G[0], g_bu, g_bv, g_south_v
+        masked = None
+        if raw:
+            bu, bv, g_bu, g_bv = X[3] * bu, X[4] * bv, G[3] * g_bu, G[4] * g_bv
+            south_v, g_south_v = southern(bv, g_bv)
+            masked = bu, bv, south_v, g_bu, g_bv, g_south_v
+        for n in range(NSUB):
+            carry = substep(carry, masked if n == 0 else None)
         for k in range(3):
             out[k, ...] = carry[k][own, 0:ny]
 
-    for k, f in enumerate((4, 5, 7)):
-        D[k] = roll(X[f], 1, 1)
-        F[k] = roll(G[f], 1, 1)
     masks = X[3, own, 0:ny], X[4, own, 0:ny]
     h_ref, u_ref, v_ref = thick, vel_u, vel_v
     n_h, n_u, n_v = mid_h, mid_u, mid_v
     for step in range(STEPS - 1):
-        substeps(X.at[0:3, own, 0:ny])
+        substeps(X.at[0:3, own, 0:ny], step == 0)
         pack_rows(step + 1, 0, 3)
         tile = send_tile(step + 1, 3)
         lead = (far_west, even)
@@ -579,6 +613,7 @@
         for _, near_copy, zz in tile[3]:
             pl.when(jnp.logical_and(top, zz == z))(near_copy.start)
         each(even, far_west, start_all, tile)
+        layer_close(n_u, n_v, sums, mean, masks, depth, step == 0)
         wait_layers(step)
         close_step(step, h_ref, v_ref, n_h, n_u, n_v)
         h_ref, u_ref, v_ref = n_h, n_u, n_v
@@ -587,7 +622,8 @@
         start_layers(out, False)
         layer_trial(h_ref, u_ref, v_ref, n_h, n_u, n_v, sums, False)
         take_tile(step + 1, 3)
-    substeps(flat)
+    substeps(flat, STEPS == 1)
+    layer_close(n_u, n_v, sums, mean, masks, depth, False)
     wait_layers(STEPS - 1)
     close_step(STEPS - 1, h_ref, v_ref, n_h, n_u, n_v)
     wait_sent()
@@ -603,6 +639,7 @@
     hbm = pl.BlockSpec(memory_space=pl.ANY)
     rows = nx + 2 * PAD
     west, east = tile_up(sum(WEST)), tile_up(sum(EAST))
+    spare = tile_up(sum(EAST) % 8 * ny // LANES)
     plane = jax.ShapeDtypeStruct((nx, ny), f32)
     solid = jax.ShapeDtypeStruct((layers, nx, ny), f32)
     kept = [(3, nx, ny), (layers, nx, ny), (layers, nx, ny), (layers, nx, ny)]
@@ -628,14 +665,16 @@
             pltpu.VMEM((2, nx, ny), f32),
             pltpu.VMEM((FIELDS, rows, ny + LANES), f32),
             pltpu.VMEM((FIELDS, rows, LANES), f32),
-            pltpu.VMEM((3, rows, ny + LANES), f32),
-            pltpu.VMEM((3, rows, LANES), f32),
+            pltpu.VMEM((6, rows, ny + LANES), f32),
+            pltpu.VMEM((6, rows, LANES), f32),
             pltpu.VMEM((2, rows, ny + LANES), f32),
             pltpu.VMEM((2, rows, LANES), f32),
             pltpu.VMEM((STEPS, west, ny), f32),
             pltpu.VMEM((STEPS, west, ny), f32),
             pltpu.VMEM((STEPS, east, ny), f32),
             pltpu.VMEM((STEPS, east, ny), f32),
+            pltpu.VMEM((spare, LANES), f32),
+            pltpu.VMEM((spare, LANES), f32),
             pltpu.VMEM((STEPS, 3, nx, LANES), f32),
             pltpu.VMEM((STEPS, rows, LANES), f32),
             pltpu.VMEM((STEPS, rows, LANES), f32),

time: 21 us -> 20.9 us (level)
  no operation moved by 1% of the time
where the time goes in v3:
time: 20.9 us; the launch traced here: 20.7 us
  Pallas kernels  20.1 us (96%)
  between operations  0.64 us (3%)
    pallas_call x1, Pallas kernels, body(): pl.pallas_call(functools.partial(kernel, zonal_devices, merid_devices), o...  18.9 us
    pallas_call x1, Pallas kernels, body(): pl.pallas_call(last_kernel, out_shape=(plane, plane, plane, solid, solid,...  1.14 us

profile of v3, /device:TPU:0, one launch (start us, length us, event | category | flops | bytes accessed | tf_op | source)
XLA Modules:
  0.0 20.7 jit_solution(10372878594403580711)
XLA Ops:
  0.6 18.9 %ocean.1 = (f32[3,16,512]{2,1,0:T(8,128)S(1)}, f32[14,16,512]{2,1,0:T(8,128)S(1)}, f32[14,16,512]{2,1,0:T(8,128)S(1)}, f32[14,16,512]{2,1,0:T(8,128)S(1)}) custom-call(f32[16,512]{1,0:T(8,128)} %height_any.1, f32[16,512]{1,0:T(8,128)} %trans_u_any.1, f32[16,512]{1,0:T(8,128)} %trans_v_any.1, f32[14,16,512]{2,1,0:T(8,128)} %thick_any.1, ...), custom_call_target="tpu_custom_call" | custom-call | tf_op jit(solution)/shard_map/ocean/pallas_call | solution.py:649
  19.6 1.1 %last.1 = (f32[16,512]{1,0:T(8,128)}, f32[16,512]{1,0:T(8,128)}, f32[16,512]{1,0:T(8,128)}, f32[14,16,512]{2,1,0:T(8,128)}, f32[14,16,512]{2,1,0:T(8,128)}, /*index=5*/f32[14,16,512]{2,1,0:T(8,128)}) custom-call(f32[3,16,512]{2,1,0:T(8,128)S(1)} %get-tuple-element.10.flat, f32[14,16,512]{2,1,0:T(8,128)S(1)} %get-tuple-element.11.n_h, ...), custom_call_target="tpu_custom_call" | custom-call | tf_op jit(solution)/shard_map/last/pallas_call | solution.py:699

commit v4 on v3

--- a/solution.py
+++ b/solution.py
@@ -342,7 +342,7 @@
         def rows_of(src, dst, k, zz, count):
             cuts = [0, CUT, count] if count > CUT else [0, count]
             parts = [slice(low, high) for low, high in zip(cuts[:-1], cuts[1:])]
-            return [send(src.at[step, p], dst.at[step, p], k, zz, m) for p in parts]
+            return [send(src.at[step, p], dst.at[step, p], 5 * k if n else k, zz, m) for n, p in enumerate(parts)]
 
         tail, whole, start = slice(nx - PAD, nx), slice(0, nx), slice(0, PAD)
         places = (slice(0, PAD), own, slice(PAD + nx, rows))
@@ -350,9 +350,9 @@
         west = rows_of(west_send, west_recv, 0, right, tile_up(sum(WEST[:fields])))
         east = rows_of(east_send, east_recv, int(step == 0), left, tile_up(sum(EAST[:fields])) if step else full_east)
         if not step:
-            east.append(send(spare_send, spare_recv, 1, left, m))
+            east.append(send(spare_send, spare_recv, 5, left, m))
         west.append(send(*inner(0, tail), 0, right, other))
-        east.append(send(*inner(2, start), int(step == 0), left, other))
+        east.append(send(*inner(2, start), 0 if step else 5, left, other))
         across = send(*inner(1, whole), 0, z, other)
         folds = []
         for s, part, zz in ((2, start, mirror_w), (1, whole, mirror), (0, tail, mirror_e)):
@@ -414,8 +414,8 @@
     X[5, own, 0:ny] = (WAVE_LIMIT / layers) * total
     pack_rows(0, FIELDS - 1, FIELDS)
     pack_edges(0, FIELDS)
-    each(*lead, lambda c: start_all(c[1:]), tile)
-    each(far_east, jnp.logical_and(far_west, jnp.logical_not(last_z)), start_all, tile)
+    each(*lead, lambda c: start_all(c[:0:-1]), tile)
+    each(far_east, jnp.logical_and(far_west, jnp.logical_not(last_z)), lambda c: start_all(c[::-1]), tile)
     tile[2].start()
     start_folds(tile[3], lambda zz: zz < z)
     for _, near_copy, zz in tile[3]:
@@ -475,6 +475,7 @@
     def wait_sent():
         drain(blank.at[0 : leaving[0]], send_sem.at[0])
         pl.when(jnp.logical_not(first_z))(lambda: drain(blank.at[0 : leaving[1]], send_sem.at[1]))
+        pl.when(jnp.logical_not(first_top))(lambda: drain(blank.at[0 : leaving[5]], send_sem.at[5]))
         for k, zz in zip((4, 3, 2), mirrors):
             pl.when(jnp.logical_and(top, zz != z))(lambda k=k: drain(blank.at[0 : leaving[k]], send_sem.at[k]))
 
@@ -518,7 +519,7 @@
     @pl.when(late_left)
     def _():
         pl.semaphore_wait(late_sem.at[0], 2)
-        start_all(tile[1])
+        start_all(tile[1][-1:] + tile[1][:-1])
 
 
     @pl.when(jnp.logical_and(top, upper > 0))
@@ -532,6 +533,8 @@
     def _():
         drain(blank.at[0 : leaving[1]], send_sem.at[1])
 
+    first_top = jnp.logical_and(first_z, top)
+    pl.when(first_top)(lambda: drain(blank.at[0 : leaving[5]], send_sem.at[5]))
     pl.when(late_left)(out[1].start)
 
     take_tile(0, FIELDS)
@@ -602,17 +605,16 @@
         pack_rows(step + 1, 0, 3)
         tile = send_tile(step + 1, 3)
         lead = (far_west, even)
-        each(*lead, lambda c: start_all(c[:-1]), tile)
 
         def inner_ready():
-            each(*lead, lambda c: c[-1].start(), tile)
+            each(*lead, lambda c: start_all(c[::-1]), tile)
             tile[2].start()
 
         pack_edges(step + 1, 3, inner_ready)
         start_folds(tile[3], lambda zz: zz != z)
         for _, near_copy, zz in tile[3]:
             pl.when(jnp.logical_and(top, zz == z))(near_copy.start)
-        each(even, far_west, start_all, tile)
+        each(even, far_west, lambda c: start_all(c[::-1]), tile)
         layer_close(n_u, n_v, sums, mean, masks, depth, step == 0)
         wait_layers(step)
         close_step(step, h_ref, v_ref, n_h, n_u, n_v)
@@ -686,7 +688,7 @@
             pltpu.VMEM((STEPS, 2, nx, LANES), f32),
             pltpu.VMEM((4 * (west + east) * ny // LANES, LANES), f32),
             pltpu.SemaphoreType.DMA((5,)),
-            pltpu.SemaphoreType.DMA((5,)),
+            pltpu.SemaphoreType.DMA((6,)),
             pltpu.SemaphoreType.DMA((STEPS,)),
             pltpu.SemaphoreType.DMA((STEPS,)),
             pltpu.SemaphoreType.REGULAR((2,)),

time: 20.9 us -> 20.5 us (0.981)
  Pallas kernels: 20.1 us -> 19.7 us
    pallas_call x1, Pallas kernels: 18.9 us -> 18.6 us  [body(): pl.pallas_call(functools.partial(kernel, zonal_devices, merid_devices), o...]
where the time goes in v4:
time: 20.5 us; the launch traced here: 20.3 us
  Pallas kernels  19.7 us (96%)
  between operations  0.64 us (3%)
    pallas_call x1, Pallas kernels, body(): pl.pallas_call(functools.partial(kernel, zonal_devices, merid_devices), o...  18.6 us
    pallas_call x1, Pallas kernels, body(): pl.pallas_call(last_kernel, out_shape=(plane, plane, plane, solid, solid,...  1.14 us

profile of v4, /device:TPU:0, one launch (start us, length us, event | category | flops | bytes accessed | tf_op | source)
XLA Modules:
  0.0 20.3 jit_solution(12356711652129134407)
XLA Ops:
  0.6 18.6 %ocean.1 = (f32[3,16,512]{2,1,0:T(8,128)S(1)}, f32[14,16,512]{2,1,0:T(8,128)S(1)}, f32[14,16,512]{2,1,0:T(8,128)S(1)}, f32[14,16,512]{2,1,0:T(8,128)S(1)}) custom-call(f32[16,512]{1,0:T(8,128)} %height_any.1, f32[16,512]{1,0:T(8,128)} %trans_u_any.1, f32[16,512]{1,0:T(8,128)} %trans_v_any.1, f32[14,16,512]{2,1,0:T(8,128)} %thick_any.1, ...), custom_call_target="tpu_custom_call" | custom-call | tf_op jit(solution)/shard_map/ocean/pallas_call | solution.py:651
  19.2 1.1 %last.1 = (f32[16,512]{1,0:T(8,128)}, f32[16,512]{1,0:T(8,128)}, f32[16,512]{1,0:T(8,128)}, f32[14,16,512]{2,1,0:T(8,128)}, f32[14,16,512]{2,1,0:T(8,128)}, /*index=5*/f32[14,16,512]{2,1,0:T(8,128)}) custom-call(f32[3,16,512]{2,1,0:T(8,128)S(1)} %get-tuple-element.10.flat, f32[14,16,512]{2,1,0:T(8,128)S(1)} %get-tuple-element.11.n_h, ...), custom_call_target="tpu_custom_call" | custom-call | tf_op jit(solution)/shard_map/last/pallas_call | solution.py:701

commit v5 on v4

--- a/solution.py
+++ b/solution.py
@@ -25,7 +25,7 @@
 WEST = (NSUB - 1, NSUB, NSUB - 1, NSUB - 1, NSUB - 2, NSUB - 1, NSUB - 1, NSUB - 2)
 EAST = (NSUB, NSUB, NSUB) + (NSUB - 1,) * 5
 ORDER = (0, 1, 2, 3, 4, 6, 7, 5)
-CUT = 32
+CUT = 24
 MESH = pl.DeviceIdType.MESH
 
 

time: 20.5 us -> 20.5 us (level)
  no operation moved by 1% of the time
where the time goes in v5:
time: 20.5 us; the launch traced here: 20.3 us
  Pallas kernels  19.7 us (96%)
  between operations  0.64 us (3%)
    pallas_call x1, Pallas kernels, body(): pl.pallas_call(functools.partial(kernel, zonal_devices, merid_devices), o...  18.6 us
    pallas_call x1, Pallas kernels, body(): pl.pallas_call(last_kernel, out_shape=(plane, plane, plane, solid, solid,...  1.14 us

profile of v5, /device:TPU:0, one launch (start us, length us, event | category | flops | bytes accessed | tf_op | source)
XLA Modules:
  0.0 20.3 jit_solution(1523868421622367418)
XLA Ops:
  0.6 18.6 %ocean.1 = (f32[3,16,512]{2,1,0:T(8,128)S(1)}, f32[14,16,512]{2,1,0:T(8,128)S(1)}, f32[14,16,512]{2,1,0:T(8,128)S(1)}, f32[14,16,512]{2,1,0:T(8,128)S(1)}) custom-call(f32[16,512]{1,0:T(8,128)} %height_any.1, f32[16,512]{1,0:T(8,128)} %trans_u_any.1, f32[16,512]{1,0:T(8,128)} %trans_v_any.1, f32[14,16,512]{2,1,0:T(8,128)} %thick_any.1, ...), custom_call_target="tpu_custom_call" | custom-call | tf_op jit(solution)/shard_map/ocean/pallas_call | solution.py:651
  19.2 1.1 %last.1 = (f32[16,512]{1,0:T(8,128)}, f32[16,512]{1,0:T(8,128)}, f32[16,512]{1,0:T(8,128)}, f32[14,16,512]{2,1,0:T(8,128)}, f32[14,16,512]{2,1,0:T(8,128)}, /*index=5*/f32[14,16,512]{2,1,0:T(8,128)}) custom-call(f32[3,16,512]{2,1,0:T(8,128)S(1)} %get-tuple-element.10.flat, f32[14,16,512]{2,1,0:T(8,128)S(1)} %get-tuple-element.11.n_h, ...), custom_call_target="tpu_custom_call" | custom-call | tf_op jit(solution)/shard_map/last/pallas_call | solution.py:701
